TPU v7x, 256 devices: a whole 4x4x8 slice. The times are simulated.
256 devices in a mesh: batch: 4 (over x), proto: 64 (over y, z, core).
Axes of the slice: x: 4, y: 4, z: 8, core: 2. Of those that a mesh axis runs over, the one named last changes fastest.
Arguments:
- view_codes: bfloat16 [4096, 1024], P('batch', 'proto'), may hold values from -80 to 80
- predictor_view_embeddings: bfloat16 [4096, 1024], P('batch', 'proto'), may hold values from -80 to 80
- prototypes: bfloat16 [65536, 1024], P('proto'), may hold values from -64 to 64
Outputs:
- assignments: bfloat16 [4096, 65536], P('batch', 'proto')
- loss_rows: float32 [4096], P('batch')
All inputs are finite; a program needn't handle non-finite values.
Results may differ from a plain program's by a relative error of at most 0.0034.
Values may be sent and summed in bfloat16 or wider, within the bound.
A program may use at most 64 MiB of HBM per device.

v0:
```python
import jax
import jax.numpy as jnp
from jax import lax
from jax.sharding import PartitionSpec as P

SINK_ITERS = 3


EPSILON = 0.05
SOFTMAX_TEMP_VALUE = 0.1


def copy_for_each(shard, axis):
    copies = jnp.broadcast_to(shard, (lax.axis_size(axis), *shard.shape))
    return lax.all_to_all(copies, axis, split_axis=0, concat_axis=0, tiled=True)


def of_everyone(shard, axis):
    return copy_for_each(shard, axis).sum(axis=0)


def together(arrays, axis):
    ravelled, at, gathered = (jnp.concatenate([a.reshape(-1) for a in arrays]), 0, [])
    subtotal = of_everyone(ravelled, axis)
    for a in arrays:
        gathered.append(subtotal[at : at + a.size].reshape(a.shape))
        at += a.size
    return tuple(gathered)


def normalized(prototypes):
    weights = prototypes.astype(jnp.float32)
    return (weights * lax.rsqrt(jnp.sum(weights * weights, axis=1, keepdims=True) + 1e-06)).astype(
        jnp.bfloat16
    )


def view_scores(embedded, unit_prototype_rows):
    products = jnp.dot(embedded, unit_prototype_rows.T, preferred_element_type=jnp.float32)
    values = embedded.astype(jnp.float32)
    inverse_factor = lax.rsqrt(jnp.sum(values * values, axis=1) + 1e-06)
    return products * inverse_factor[:, None]


def local(view_codes, predictor_view_embeddings, prototypes):
    unit_prototype_rows = normalized(prototypes)
    whole_first, whole_second = (
        lax.all_gather(view_codes, "proto", axis=1, tiled=True),
        lax.all_gather(predictor_view_embeddings, "proto", axis=1, tiled=True),
    )
    scores_codes = view_scores(whole_first, unit_prototype_rows)
    predictor_scores = view_scores(whole_second, unit_prototype_rows)
    kernel = jnp.exp(scores_codes / EPSILON)
    rows_total = kernel.shape[0] * lax.axis_size("batch")
    protos_total = kernel.shape[1] * lax.axis_size("proto")
    logit_scores = predictor_scores / SOFTMAX_TEMP_VALUE
    scale_rows = jnp.ones((kernel.shape[0],), jnp.float32)
    for iteration in range(SINK_ITERS):
        col_part = jnp.dot(scale_rows, kernel, precision=lax.Precision.HIGHEST)
        col_sums = of_everyone(col_part, "batch")
        scale_cols = 1.0 / (protos_total * col_sums)
        row_part = jnp.dot(kernel, scale_cols, precision=lax.Precision.HIGHEST)
        row_sums = of_everyone(row_part, "proto")
        scale_rows = 1.0 / (rows_total * row_sums)
    assign = kernel * scale_cols[None, :] * (rows_total * scale_rows)[:, None]
    assignments = (protos_total * assign).astype(jnp.bfloat16)
    cross_part = jnp.sum(assign * logit_scores, axis=1)
    totals, cross_term = together((jnp.sum(jnp.exp(logit_scores), axis=1), cross_part), "proto")
    loss_rows = jnp.log(totals) - cross_term
    return (assignments, loss_rows)


def solution(mesh):
    placed = (P("batch", "proto"), P("batch", "proto"), P("proto", None))
    return jax.shard_map(
        local,
        mesh=mesh,
        in_specs=placed,
        out_specs=(P("batch", "proto"), P("batch")),
        check_vma=False,
    )
```

profile of v0, /device:TPU:1, one launch (start us, length us, event | category | flops | bytes accessed | tf_op | source)
XLA Modules:
  0.0 249.5 jit_solution(1705991306893637967)
XLA Ops:
  8.7 2.1 fusion
  10.7 81.8 %all-gather.3.cloned.1.call-done = bf16[1024,1024]{0,1:T(8,128)(2,1)} async-done(((bf16[1024,16]{0,1:T(8,128)(2,1)}), bf16[1024,1024]{0,1:T(8,128)(2,1)}) %all-gather.3.cloned.1.call-update) | async-done | bytes 2097168 | tf_op jit(solution)/shard_map/all_gather | solution.py:48
  92.6 2.1 multiply_reduce_fusion.1
  94.7 4.0 %multiply_exponential_fusion = f32[1024,1024]{1,0:T(8,128)S(1)} fusion(bf16[1024,1024]{0,1:T(8,128)(2,1)} %all-gather.3.cloned.1.call-done, f32[1024]{0:T(1024)S(1)} %add_rsqrt_fusion.1, bf16[1024,1024]{1,0:T(8,128)(2,1)S(1)} %copy-done.1, f32[1024]{0:T(1024)S(1)} %add_rsqrt_fusion.2), kind=kOutput, calls=%fused_computation.25 | convolution fusion | flops 2152726528 | bytes 8396800 | tf_op jit(solution)/shard_map/dot_general | solution.py:39
  98.7 1.9 copy-done
  100.6 3.6 %fusion.14 = f32[1,1024]{1,0:T(1,128)S(1)} fusion(f32[1024,1024]{1,0:T(8,128)S(1)} %multiply_exponential_fusion), kind=kOutput, calls=%fused_computation.19 | convolution fusion | flops 12582912 | bytes 4198400 | tf_op jit(solution)/shard_map/dot_general | solution.py:59
  104.2 8.1 %all_to_all.42 = f32[4,1,1024]{2,1,0:T(1,128)S(1)} all-to-all(f32[4,1,1024]{2,1,0:T(1,128)S(1)} %broadcast_in_dim.26), channel_id=1, replica_groups=mesh['batch'=4,'proto'=64] {'batch'}, dimensions={0} | all-to-all | bytes 32768 | tf_op jit(solution)/shard_map/all_to_all | solution.py:15
  112.2 4.4 %fusion.12 = f32[1,1024]{1,0:T(1,128)S(1)} fusion(f32[1024,1]{0,1:T(1,128)S(1)} %bitcast.52, f32[1024,1024]{1,0:T(8,128)} %copy-done), kind=kOutput, calls=%fused_computation.17 | convolution fusion | flops 12582912 | bytes 4202496 | tf_op jit(solution)/shard_map/dot_general | solution.py:62
  116.8 19.7 %all_to_all.43 = f32[64,1,1024]{2,1,0:T(1,128)S(1)} all-to-all(f32[64,1,1024]{2,1,0:T(1,128)S(1)} %broadcast_in_dim.27), channel_id=1, replica_groups=mesh['batch'=4,'proto'=64] {'proto'}, dimensions={0} | all-to-all | bytes 524288 | tf_op jit(solution)/shard_map/all_to_all | solution.py:15
  136.7 5.6 %fusion.10 = f32[1,1024]{1,0:T(1,128)S(1)} fusion(f32[1024,1]{0,1:T(1,128)S(1)} %bitcast.53, f32[1024,1024]{1,0:T(8,128)} %copy-done), kind=kOutput, calls=%fused_computation.15 | convolution fusion | flops 12582912 | bytes 4202496 | tf_op jit(solution)/shard_map/dot_general | solution.py:59
  142.4 6.6 %all_to_all.44 = f32[4,1,1024]{2,1,0:T(1,128)S(1)} all-to-all(f32[4,1,1024]{2,1,0:T(1,128)S(1)} %broadcast_in_dim.28), channel_id=1, replica_groups=mesh['batch'=4,'proto'=64] {'batch'}, dimensions={0} | all-to-all | bytes 32768 | tf_op jit(solution)/shard_map/all_to_all | solution.py:15
  149.0 4.4 %fusion.8 = f32[1,1024]{1,0:T(1,128)S(1)} fusion(f32[1024,1]{0,1:T(1,128)S(1)} %bitcast.54, f32[1024,1024]{1,0:T(8,128)} %copy-done), kind=kOutput, calls=%fused_computation.13 | convolution fusion | flops 12582912 | bytes 4202496 | tf_op jit(solution)/shard_map/dot_general | solution.py:62
  153.6 19.1 %all_to_all.45 = f32[64,1,1024]{2,1,0:T(1,128)S(1)} all-to-all(f32[64,1,1024]{2,1,0:T(1,128)S(1)} %broadcast_in_dim.29), channel_id=1, replica_groups=mesh['batch'=4,'proto'=64] {'proto'}, dimensions={0} | all-to-all | bytes 524288 | tf_op jit(solution)/shard_map/all_to_all | solution.py:15
  172.8 5.6 %fusion.6 = f32[1,1024]{1,0:T(1,128)S(1)} fusion(f32[1024,1]{0,1:T(1,128)S(1)} %bitcast.55, f32[1024,1024]{1,0:T(8,128)} %copy-done), kind=kOutput, calls=%fused_computation.11 | convolution fusion | flops 12582912 | bytes 4202496 | tf_op jit(solution)/shard_map/dot_general | solution.py:59
  178.5 6.6 %all_to_all.46 = f32[4,1,1024]{2,1,0:T(1,128)S(1)} all-to-all(f32[4,1,1024]{2,1,0:T(1,128)S(1)} %broadcast_in_dim.30), channel_id=1, replica_groups=mesh['batch'=4,'proto'=64] {'batch'}, dimensions={0} | all-to-all | bytes 32768 | tf_op jit(solution)/shard_map/all_to_all | solution.py:15
  185.1 4.4 %fusion.4 = f32[1,1024]{1,0:T(1,128)S(1)} fusion(f32[1024,1]{0,1:T(1,128)S(1)} %bitcast.51, f32[1024,1024]{1,0:T(8,128)} %copy-done), kind=kOutput, calls=%fused_computation.8 | convolution fusion | flops 12582912 | bytes 4202496 | tf_op jit(solution)/shard_map/dot_general | solution.py:62
  190.4 7.9 %all-to-all-start.5 = ((f32[64,1,1024]{2,1,0:T(1,128)}), f32[64,1,1024]{2,1,0:T(1,128)S(1)}, u32[]{:S(2)}, u32[]{:S(2)}) async-start(f32[64,1,1024]{2,1,0:T(1,128)} %broadcast_in_dim.31), calls=%async_computation.5 | async-start | bytes 524288 | tf_op jit(solution)/shard_map/all_to_all | solution.py:15
  198.3 2.1 multiply_reduce_fusion
  200.4 9.9 %all-to-all-done.5 = f32[64,1,1024]{2,1,0:T(1,128)S(1)} async-done(((f32[64,1,1024]{2,1,0:T(1,128)}), f32[64,1,1024]{2,1,0:T(1,128)S(1)}, u32[]{:S(2)}, u32[]{:S(2)}) %all-to-all-start.5) | async-done | bytes 262176 | tf_op jit(solution)/shard_map/all_to_all | solution.py:15
  210.5 6.9 %fusion.2 = (f32[1024]{0:T(1024)S(1)}, f32[1024]{0:T(1024)S(1)}, bf16[1024,1024]{0,1:T(8,128)(2,1)}) fusion(f32[1024]{0:T(1024)S(1)} %add_rsqrt_fusion, f32[1024]{0:T(1024)S(1)} %divide_multiply_fusion, f32[1024]{0:T(1024)S(1)} %multiply_divide_fusion, f32[1024,1024]{1,0:T(8,128)} %copy-done, bf16[1024,1024]{0,1:T(8,128)(2,1)} %all-gather.5.cloned.1.call-done, ...), kind=kOutput, calls=%fused_computation.6 | convolution fusion | flops 2160064512 | bytes 10510336 | tf_op jit(solution)/shard_map/dot_general | solution.py:39
  217.3 1.1 broadcast_in_dim.32
  218.4 6.0 %all-to-all-start.6 = ((f32[64,1,2048]{2,1,0:T(1,128)}), f32[64,1,2048]{2,1,0:T(1,128)S(1)}, u32[]{:S(2)}, u32[]{:S(2)}) async-start(f32[64,1,2048]{2,1,0:T(1,128)} %broadcast_in_dim.32), calls=%async_computation.6 | async-start | bytes 1048576 | tf_op jit(solution)/shard_map/all_to_all | solution.py:15
  224.4 3.9 %copy.14 = bf16[1024,1024]{1,0:T(8,128)(2,1)} copy(bf16[1024,1024]{0,1:T(8,128)(2,1)} %get-tuple-element.10) | data formatting | bytes 4194304
  228.4 13.3 %all-to-all-done.6 = f32[64,1,2048]{2,1,0:T(1,128)S(1)} async-done(((f32[64,1,2048]{2,1,0:T(1,128)}), f32[64,1,2048]{2,1,0:T(1,128)S(1)}, u32[]{:S(2)}, u32[]{:S(2)}) %all-to-all-start.6) | async-done | bytes 524320 | tf_op jit(solution)/shard_map/all_to_all | solution.py:15
  (32 shorter events, 4.3 us)
Async XLA Ops:
  7.2 87.5 %copy-start.1 = (bf16[1024,1024]{1,0:T(8,128)(2,1)S(1)}, bf16[1024,1024]{1,0:T(8,128)(2,1)}, u32[]{:S(2)}) copy-start(bf16[1024,1024]{1,0:T(8,128)(2,1)} %param.5) | copy-start | bytes 6291460
  7.2 85.4 %all-gather.3.cloned.1.call-start = ((), (), s32[]{:S(2)}) async-start(), calls=%async_computation.7 | async-start | bytes 2129920 | tf_op jit(solution)/shard_map/all_gather | solution.py:48
  7.9 190.4 %all-gather.5.cloned.1.call-start = ((), (), s32[]{:S(2)}) async-start(), calls=%async_computation.8 | async-start | bytes 2129920 | tf_op jit(solution)/shard_map/all_gather | solution.py:49
  98.6 1.9 copy-start
  190.4 19.9 %all-to-all-start.5 = ((f32[64,1,1024]{2,1,0:T(1,128)}), f32[64,1,1024]{2,1,0:T(1,128)S(1)}, u32[]{:S(2)}, u32[]{:S(2)}) async-start(f32[64,1,1024]{2,1,0:T(1,128)} %broadcast_in_dim.31), calls=%async_computation.5 | async-start | bytes 524288 | tf_op jit(solution)/shard_map/all_to_all | solution.py:15
  218.4 23.3 %all-to-all-start.6 = ((f32[64,1,2048]{2,1,0:T(1,128)}), f32[64,1,2048]{2,1,0:T(1,128)S(1)}, u32[]{:S(2)}, u32[]{:S(2)}) async-start(f32[64,1,2048]{2,1,0:T(1,128)} %broadcast_in_dim.32), calls=%async_computation.6 | async-start | bytes 1048576 | tf_op jit(solution)/shard_map/all_to_all | solution.py:15
Sparse Core Ops, SparseCore 0:
  10.8 81.7 all-gather.2
  95.3 75.9 all-gather.4
where the time goes:
time: 250 us; the launch traced here: 249 us
  waiting for transfers between devices  106 us (42%)
  blocking collectives  59.9 us (24%)
  matrix products  39 us (16%)
  between operations  14.2 us (6%)
  starting transfers between devices  14 us (6%)
  local copies, waits for them, and re-layouts  8.12 us (3%)
  other arithmetic  7.8 us (3%)
    all_gather x1, waiting for transfers between devices, local(): lax.all_gather(view_codes, 'proto', axis=1, tiled=True)  81.8 us
    all_to_all x5, blocking collectives, copy_for_each(): return lax.all_to_all(copies, axis, split_axis=0, concat_axis=0, tiled=True)  59.9 us
    all_to_all x2, waiting for transfers between devices, copy_for_each(): return lax.all_to_all(copies, axis, split_axis=0, concat_axis=0, tiled=True)  23.2 us
    dot_general x3, matrix products, local(): col_part = jnp.dot(scale_rows, kernel, precision=lax.Precision.HIGHEST)  14.9 us
    all_to_all x2, starting transfers between devices, copy_for_each(): return lax.all_to_all(copies, axis, split_axis=0, concat_axis=0, tiled=True)  13.9 us
    dot_general x3, matrix products, local(): row_part = jnp.dot(kernel, scale_cols, precision=lax.Precision.HIGHEST)  13.3 us
    dot_general x2, matrix products, view_scores(): jnp.dot(embedded, unit_prototype_rows.T, preferred_element_type=jnp.float32)  10.9 us
    unnamed x5, local copies, waits for them, and re-layouts  5.86 us
  transfers between devices with their start and end apart: 4, of which 3 were waited for; matrix products, arithmetic and copies ran while one was open for 18% of the time, Pallas kernels for 0%

commit v1 on v0

v1 whole, which is shorter than its diff:
```python
import functools
import math

import jax
import jax.numpy as jnp
from jax import lax
from jax.experimental import pallas as pl
from jax.experimental.pallas import tpu as pltpu
from jax.sharding import PartitionSpec as P

SINK_ITERS = 3
EPSILON = 0.05
SOFTMAX_TEMP_VALUE = 0.1
LOG2E = math.log2(math.e)

MESH = pl.DeviceIdType.MESH
NX, NY, NZ = 4, 4, 8
NCHIP = NY * NZ
ROWS = 1024
COLS = 1024
DIM = 1024
SHARD = 16
LANES = 128
TOTAL_ROWS = 4096
TOTAL_PROTOS = 65536


def swap_kernel(
    v1_ref, v2_ref, p_ref, out_ref, loss_ref,
    xg, xp, praw, pu, kern, s2, xb, col_r, inv_col,
    colbuf, rowbuf, xbuf, cvec, svec, rvec, lvec, sstat, pstat, inv_row2,
    local_sem, stage_sem, gather_rs, send_sem, xp_rs, pu_rs, col_rs, row_rs, x_rs, vec_rs,
):
    b = lax.axis_index("batch")
    q = lax.axis_index("proto")
    c = q % 2
    z = (q // 2) % NZ
    y = q // (2 * NZ)
    chip = y * NZ + z

    def device(bb, yy, zz, cc):
        return (bb, yy * (2 * NZ) + zz * 2 + cc)

    def at_y(d):
        return device(b, (y + d) % NY, z, c)

    def at_z(d):
        return device(b, y, (z + d) % NZ, c)

    partner = device(b, y, z, 1 - c)
    sent = []

    def remote(src, dst, rsem, dev):
        return pltpu.make_async_remote_copy(
            src_ref=src, dst_ref=dst, send_sem=send_sem, recv_sem=rsem,
            device_id=dev, device_id_type=MESH)

    def start(src, dst, rsem, dev):
        copy = remote(src, dst, rsem, dev)
        copy.start()
        sent.append(copy)

    def drain():
        for copy in sent:
            copy.wait_send()
        sent.clear()

    own_p = pltpu.make_async_copy(p_ref, praw, local_sem.at[0])
    own_p.start()

    barrier = pltpu.get_barrier_semaphore()
    greet = [partner]
    greet += [device((b + d) % NX, y, z, c) for d in range(1, NX)]
    greet += [at_y(d) for d in range(1, NY)]
    greet += [at_z(d) for d in range(1, NZ)]
    for dev in greet:
        pl.semaphore_signal(barrier, 1, device_id=dev, device_id_type=MESH)
    pl.semaphore_wait(barrier, len(greet))

    def normalize(slot):
        own_p.wait()

        def body(i, _):
            rows = pl.ds(pl.multiple_of(i * 64, 64), 64)
            w = praw[rows, :].astype(jnp.float32)
            total = jnp.sum(w * w, axis=1, keepdims=True)
            pu[slot, rows, :] = (w * lax.rsqrt(total + 1e-06)).astype(jnp.bfloat16)
            return 0

        lax.fori_loop(0, ROWS // 64, body, 0)

    def put(yy, zz, h, dev):
        start(xg.at[yy, zz, h], xg.at[yy, zz, h], gather_rs.at[yy, zz, h], dev)

    def arrived(yy, zz, h):
        remote(xg.at[yy, zz, h], xg.at[yy, zz, h], gather_rs.at[yy, zz, h], partner).wait_recv()

    def hops(j, direction):
        far = NZ // 2
        if direction > 0:
            return far if j in (0, 1) else far - 1
        return far - 1 if j in (0, 1) else far

    def gather():
        def yj(j):
            return (y + j) % NY

        def zk(k):
            return (z + k) % NZ

        for d in (2, 1, 3):
            put(y, z, 0, at_y(d))
        for h in (0, 1):
            put(y, z, h, at_z(1))
            put(y, z, h, at_z(-1 + NZ))
        for d in (2, 1, 3):
            put(y, z, 1, at_y(d))

        def ring(k, js):
            for direction in (1, -1):
                zz = zk(NZ - k) if direction > 0 else zk(k)
                nxt = at_z(1) if direction > 0 else at_z(NZ - 1)
                for j in js:
                    if hops(j, direction) >= k:
                        arrived(yj(j), zz, 0)
                        if hops(j, direction) > k:
                            put(yj(j), zz, 0, nxt)
                    if j == 0 and hops(1, direction) >= k:
                        arrived(y, zz, 1)
                        if hops(1, direction) > k:
                            put(y, zz, 1, nxt)
                        for d in (2, 1, 3):
                            put(y, zz, 1, at_y(d))

        far = NZ // 2
        ring(1, (0,))
        for j in (1, 3, 2):
            arrived(yj(j), z, 0)
            put(yj(j), z, 0, at_z(1))
            put(yj(j), z, 0, at_z(NZ - 1))
        for k in range(1, far + 1):
            if k < far:
                ring(k + 1, (0,))
            ring(k, (1, 3, 2))
        for zz in range(NZ):
            for j in (1, 2, 3):
                arrived(yj(j), zk(zz), 1)

    def inverse_norms(xt):
        def body(s, acc):
            v = xt[s // NZ, s % NZ].reshape(2 * SHARD, ROWS).astype(jnp.float32)
            return acc + v * v

        acc = lax.fori_loop(0, NCHIP, body, jnp.zeros((2 * SHARD, ROWS), jnp.float32))
        return lax.rsqrt(jnp.sum(acc, axis=0, keepdims=True) + 1e-06)

    def spread(row, dst, g):
        dst[g * LANES:(g + 1) * LANES, :] = jnp.transpose(
            jnp.broadcast_to(row, (LANES, LANES)))

    def transpose_view(xt):
        for kb in range(DIM // LANES):
            yy, z0 = kb // 2, (kb % 2) * 4
            block = xt[yy, z0:z0 + 4].reshape(LANES, ROWS)
            xb[:, kb * LANES:(kb + 1) * LANES] = jnp.transpose(block)

    MB, NB = 512, 256

    def products(slot, n0, epilogue):
        def body(i, _):
            nrows = pl.ds(pl.multiple_of(i * NB, NB), NB)
            ncols = pl.ds(pl.multiple_of(n0 + i * NB, NB), NB)
            for m in range(ROWS // MB):
                mrows = slice(m * MB, (m + 1) * MB)
                s = lax.dot_general(
                    xb[mrows, :], pu[slot, nrows, :], (((1,), (1,)), ((), ())),
                    preferred_element_type=jnp.float32)
                epilogue(mrows, ncols, s)
            return 0

        lax.fori_loop(0, COLS // NB, body, 0)

    def kernel_block(xt, slots):
        inv = inverse_norms(xt) * (LOG2E / EPSILON)
        for g in range(ROWS // LANES):
            spread(inv[:, g * LANES:(g + 1) * LANES], inv_col, g)
        transpose_view(xt)

        def epilogue(mrows, ncols, s):
            scale = inv_col[mrows, :]
            for t in range(NB // LANES):
                part = s[:, t * LANES:(t + 1) * LANES]
                kern[mrows, pl.ds(pl.multiple_of(ncols.start + t * LANES, LANES), LANES)] = (
                    jnp.exp2(part * scale))

        for n, slot in enumerate(slots):
            products(slot, n * COLS, epilogue)

    def second_view(xt, slot):
        inv = inverse_norms(xt)
        for g in range(ROWS // LANES):
            piece = inv[:, g * LANES:(g + 1) * LANES]
            inv_row2[g:g + 1, :] = piece
            spread(piece * (LOG2E / SOFTMAX_TEMP_VALUE), inv_col, g)
        transpose_view(xt)

        def epilogue(mrows, ncols, s):
            s2[mrows, ncols] = s

        products(slot, 0, epilogue)

        def body(g, _):
            rows = pl.ds(pl.multiple_of(g * LANES, LANES), LANES)
            scale = inv_col[rows, :]
            acc = jnp.zeros((LANES, LANES), jnp.float32)
            for j in range(COLS // LANES):
                acc += jnp.exp2(s2[rows, j * LANES:(j + 1) * LANES] * scale)
            pstat[0, pl.ds(g, 1), :] = jnp.sum(jnp.transpose(acc), axis=0, keepdims=True)
            return 0

        lax.fori_loop(0, ROWS // LANES, body, 0)

    def column_pass(dst, first):
        def body(j, _):
            block = kern[:, pl.ds(pl.multiple_of(j * LANES, LANES), LANES)]
            if not first:
                block = block * col_r[...]
            part = jnp.sum(block.reshape(ROWS // 8, 8, LANES), axis=0)
            dst[pl.ds(j, 1), :] = jnp.sum(part, axis=0, keepdims=True)
            return 0

        lax.fori_loop(0, 2 * COLS // LANES, body, 0)

    def row_pass(dst):
        def body(g, _):
            rows = pl.ds(pl.multiple_of(g * LANES, LANES), LANES)
            acc = jnp.zeros((LANES, LANES), jnp.float32)
            for j in range(2 * COLS // LANES):
                acc += kern[rows, j * LANES:(j + 1) * LANES] * cvec[j:j + 1, :]
            dst[pl.ds(g, 1), :] = jnp.sum(jnp.transpose(acc), axis=0, keepdims=True)
            return 0

        lax.fori_loop(0, ROWS // LANES, body, 0)

    def cross_pass(k0, cref):
        def body(g, _):
            rows = pl.ds(pl.multiple_of(g * LANES, LANES), LANES)
            acc = jnp.zeros((LANES, LANES), jnp.float32)
            for j in range(COLS // LANES):
                acc += (
                    kern[rows, k0 + j * LANES:k0 + (j + 1) * LANES]
                    * cref[j:j + 1, :]
                    * s2[rows, j * LANES:(j + 1) * LANES])
            total = jnp.sum(jnp.transpose(acc), axis=0, keepdims=True)
            pstat[1, pl.ds(g, 1), :] = (
                total * inv_row2[pl.ds(g, 1), :] * (1.0 / SOFTMAX_TEMP_VALUE))
            return 0

        lax.fori_loop(0, ROWS // LANES, body, 0)

    def spread_rows(rows8):
        for g in range(ROWS // LANES):
            spread(rows8[g:g + 1, :], col_r, g)

    def write_out(k0, cref):
        def body(g, _):
            rows = pl.ds(pl.multiple_of(g * LANES, LANES), LANES)
            scale = col_r[rows, :] * float(TOTAL_ROWS)
            for j in range(COLS // LANES):
                lanes = slice(j * LANES, (j + 1) * LANES)
                assign = (
                    kern[rows, k0 + j * LANES:k0 + (j + 1) * LANES] * cref[j:j + 1, :]) * scale
                out_ref[rows, lanes] = (assign * float(TOTAL_PROTOS)).astype(jnp.bfloat16)
            return 0

        lax.fori_loop(0, ROWS // LANES, body, 0)

    def exchange_columns(it):
        for d in range(1, NX):
            start(colbuf.at[it, b], colbuf.at[it, b], col_rs.at[it],
                  device((b + d) % NX, y, z, c))
        peers = colbuf.at[it, pl.ds(0, NX - 1)]
        remote(peers, peers, col_rs.at[it], partner).wait_recv()
        total = (colbuf[it, 0] + colbuf[it, 1]) + (colbuf[it, 2] + colbuf[it, 3])
        cvec[...] = 1.0 / (float(TOTAL_PROTOS) * total)

    def plane_send(ref, rsem):
        for dy in range(NY):
            for dz in range(NZ):
                if dy or dz:
                    start(ref, ref, rsem, device(b, (y + dy) % NY, (z + dz) % NZ, c))

    def plane_wait(peers, rsem):
        remote(peers, peers, rsem, partner).wait_recv()

    @pl.when(c == 1)
    def _():
        own = pltpu.make_async_copy(v1_ref, xg.at[y, z, 1], local_sem.at[1])
        own.start()
        start(v2_ref, xg.at[y, z, 1], stage_sem, partner)
        normalize(1)
        own.wait()
        remote(v1_ref, xg.at[y, z, 0], stage_sem, partner).wait_recv()
        gather()
        start(xg, xp, xp_rs, partner)
        remote(pu.at[0], pu.at[0], pu_rs, partner).wait_recv()
        kernel_block(xg, (0, 1))
        for it in range(SINK_ITERS):
            column_pass(colbuf.at[it, b], it == 0)
            exchange_columns(it)
            if it == SINK_ITERS - 1:
                start(cvec.at[pl.ds(0, 8)], svec, vec_rs.at[0], partner)
            row_pass(rowbuf.at[it, chip])
            plane_send(rowbuf.at[it, chip], row_rs.at[it])
            if it == 1:
                remote(xg, xp, xp_rs, partner).wait_recv()
                second_view(xp, 1)
            if it == SINK_ITERS - 1:
                cross_pass(COLS, cvec.at[pl.ds(8, 8)])
                remote(pstat, sstat, vec_rs.at[1], partner).wait_recv()
                xbuf[chip] = pstat[...] + sstat[...]
                plane_send(xbuf.at[chip], x_rs)
            plane_wait(rowbuf.at[it, pl.ds(0, NCHIP - 1)], row_rs.at[it])
            row_sums = jnp.sum(rowbuf[it], axis=0)
            rvec[...] = 1.0 / (float(TOTAL_ROWS) * row_sums)
            if it == SINK_ITERS - 1:
                start(rvec, lvec.at[0], vec_rs.at[2], partner)
            spread_rows(rvec)
        write_out(COLS, cvec.at[pl.ds(8, 8)])
        plane_wait(xbuf.at[pl.ds(0, NCHIP - 1)], x_rs)
        stats = jnp.sum(xbuf[...], axis=0)
        row_sums = jnp.sum(rowbuf[SINK_ITERS - 1], axis=0)
        loss = jnp.log(stats[0]) - stats[1] / row_sums
        loss_ref[...] = loss
        lvec[1] = loss
        start(lvec.at[1], lvec.at[1], vec_rs.at[3], partner)
        drain()

    @pl.when(c == 0)
    def _():
        own = pltpu.make_async_copy(v2_ref, xg.at[y, z, 0], local_sem.at[1])
        own.start()
        start(v1_ref, xg.at[y, z, 0], stage_sem, partner)
        normalize(0)
        start(pu.at[0], pu.at[0], pu_rs, partner)
        own.wait()
        remote(v2_ref, xg.at[y, z, 1], stage_sem, partner).wait_recv()
        remote(xg, xp, xp_rs, partner).wait_recv()
        gather()
        start(xg, xp, xp_rs, partner)
        kernel_block(xp, (0,))
        second_view(xg, 0)
        remote(cvec.at[pl.ds(0, 8)], svec, vec_rs.at[0], partner).wait_recv()
        cross_pass(0, svec)
        start(pstat, sstat, vec_rs.at[1], partner)
        remote(rvec, lvec.at[0], vec_rs.at[2], partner).wait_recv()
        spread_rows(lvec.at[0])
        write_out(0, svec)
        remote(lvec.at[1], lvec.at[1], vec_rs.at[3], partner).wait_recv()
        loss_ref[...] = lvec[1]
        drain()


def local(view_codes, predictor_view_embeddings, prototypes):
    f32, bf16 = jnp.float32, jnp.bfloat16
    anywhere = pl.BlockSpec(memory_space=pl.ANY)
    vmem = pl.BlockSpec(memory_space=pltpu.VMEM)
    dma = pltpu.SemaphoreType.DMA
    assignments, loss = pl.pallas_call(
        swap_kernel,
        out_shape=(
            jax.ShapeDtypeStruct((ROWS, COLS), bf16),
            jax.ShapeDtypeStruct((8, LANES), f32),
        ),
        in_specs=[anywhere] * 3,
        out_specs=(vmem, vmem),
        scratch_shapes=[
            pltpu.VMEM((NY, NZ, 2, SHARD, ROWS), bf16),
            pltpu.VMEM((NY, NZ, 2, SHARD, ROWS), bf16),
            pltpu.VMEM((COLS, DIM), bf16),
            pltpu.VMEM((2, COLS, DIM), bf16),
            pltpu.VMEM((ROWS, 2 * COLS), f32),
            pltpu.VMEM((ROWS, COLS), f32),
            pltpu.VMEM((ROWS, DIM), bf16),
            pltpu.VMEM((ROWS, LANES), f32),
            pltpu.VMEM((ROWS, LANES), f32),
            pltpu.VMEM((SINK_ITERS, NX, 16, LANES), f32),
            pltpu.VMEM((SINK_ITERS, NCHIP, 8, LANES), f32),
            pltpu.VMEM((NCHIP, 2, 8, LANES), f32),
            pltpu.VMEM((16, LANES), f32),
            pltpu.VMEM((8, LANES), f32),
            pltpu.VMEM((8, LANES), f32),
            pltpu.VMEM((2, 8, LANES), f32),
            pltpu.VMEM((2, 8, LANES), f32),
            pltpu.VMEM((2, 8, LANES), f32),
            pltpu.VMEM((8, LANES), f32),
            dma((2,)),
            dma(()),
            dma((NY, NZ, 2)),
            dma(()),
            dma(()),
            dma(()),
            dma((SINK_ITERS,)),
            dma((SINK_ITERS,)),
            dma(()),
            dma((4,)),
        ],
        compiler_params=pltpu.CompilerParams(
            collective_id=0, has_side_effects=True, vmem_limit_bytes=48 << 20),
        name="swapped_sinkhorn",
    )(view_codes.T, predictor_view_embeddings.T, prototypes)
    return assignments, loss.reshape(ROWS)


def solution(mesh):
    placed = (P("batch", "proto"), P("batch", "proto"), P("proto", None))
    return jax.shard_map(
        local,
        mesh=mesh,
        in_specs=placed,
        out_specs=(P("batch", "proto"), P("batch")),
        check_vma=False,
    )
```

time: 250 us -> 82.1 us (0.33)
  waiting for transfers between devices: 106 us -> 0 us
  Pallas kernels: 0 us -> 76.2 us
  blocking collectives: 59.9 us -> 0 us
  matrix products: 39 us -> 0 us
  starting transfers between devices: 14 us -> 0 us
  between operations: 14.2 us -> 0.65 us
  other arithmetic: 7.8 us -> 0 us
  local copies, waits for them, and re-layouts: 8.12 us -> 5.01 us
    all_gather x2 -> x0, waiting for transfers between devices: 81.8 us -> none  [the longest x1 81.8 us: local(): lax.all_gather(view_codes, 'proto', axis=1, tiled=True)]
    pallas_call x0 -> x1, Pallas kernels: none -> 76.2 us  [local(): pl.pallas_call(swap_kernel, out_shape=(jax.ShapeDtypeStruct((ROWS, COLS),...]
    all_to_all x5 -> x0, blocking collectives: 59.9 us -> none  [copy_for_each(): return lax.all_to_all(copies, axis, split_axis=0, concat_axis=0, tiled=True)]
    dot_general x8 -> x0, matrix products: 39 us -> none  [the longest x3 14.9 us: local(): col_part = jnp.dot(scale_rows, kernel, precision=lax.Precision.HIGHEST)]
    all_to_all x2 -> x0, waiting for transfers between devices: 23.2 us -> none  [copy_for_each(): return lax.all_to_all(copies, axis, split_axis=0, concat_axis=0, tiled=True)]
    all_to_all x2 -> x0, starting transfers between devices: 13.9 us -> none  [copy_for_each(): return lax.all_to_all(copies, axis, split_axis=0, concat_axis=0, tiled=True)]
    reduce_sum x10 -> x0, other arithmetic: 7.13 us -> none  [the longest x2 4.14 us: view_scores(): inverse_factor = lax.rsqrt(jnp.sum(values * values, axis=1) + 1e-06)]
    unnamed x5 -> x8, local copies, waits for them, and re-layouts: 5.86 us -> 5.01 us
  transfers between devices with their start and end apart: 4 -> 0, of which waited for: 3 -> 0; matrix products, arithmetic and copies ran while one was open for 18% -> 0% of each run, Pallas kernels for 0% -> 0%
where the time goes in v1:
time: 82.1 us; the launch traced here: 81.8 us
  Pallas kernels  76.2 us (93%)
  local copies, waits for them, and re-layouts  5.01 us (6%)
    pallas_call x1, Pallas kernels, local(): pl.pallas_call(swap_kernel, out_shape=(jax.ShapeDtypeStruct((ROWS, COLS),...  76.2 us
    unnamed x8, local copies, waits for them, and re-layouts  5.01 us

profile of v1, /device:TPU:1, one launch (start us, length us, event | category | flops | bytes accessed | tf_op | source)
XLA Modules:
  0.0 81.8 jit_solution(6202904280655192537)
XLA Ops:
  0.6 0.0 copy-start
  0.6 1.6 %copy-done = bf16[1024,1024]{1,0:T(8,128)(2,1)S(1)} copy-done((bf16[1024,1024]{1,0:T(8,128)(2,1)S(1)}, bf16[1024,1024]{1,0:T(8,128)(2,1)}, u32[]{:S(2)}) %copy-start) | copy-done | bytes 2097176
  2.2 0.0 copy-start.1
  2.2 0.8 copy-done.1
  3.0 0.0 copy-start.2
  3.0 0.8 copy-done.2
  3.7 76.2 %swapped_sinkhorn.1 = (bf16[1024,1024]{1,0:T(8,128)(2,1)S(1)}, f32[8,128]{1,0:T(8,128)S(1)}) custom-call(bf16[16,1024]{1,0:T(8,128)(2,1)S(1)} %bitcast.3, bf16[16,1024]{1,0:T(8,128)(2,1)S(1)} %bitcast.4, bf16[1024,1024]{1,0:T(8,128)(2,1)S(1)} %copy-done), custom_call_target="tpu_custom_call" | custom-call | tf_op jit(solution)/shard_map/swapped_sinkhorn/pallas_call | solution.py:369
  79.9 1.3 %copy.7 = bf16[1024,1024]{1,0:T(8,128)(2,1)} copy(bf16[1024,1024]{1,0:T(8,128)(2,1)S(1)} %get-tuple-element.8) | data formatting | bytes 4194304
  81.3 0.6 copy.8
Async XLA Ops:
  0.6 1.6 %copy-start = (bf16[1024,1024]{1,0:T(8,128)(2,1)S(1)}, bf16[1024,1024]{1,0:T(8,128)(2,1)}, u32[]{:S(2)}) copy-start(bf16[1024,1024]{1,0:T(8,128)(2,1)} %p_ref.1) | copy-start | bytes 6291460
  2.2 0.8 copy-start.1
  3.0 0.8 copy-start.2

commit v2 on v1

v2 whole, which is shorter than its diff:
```python
import functools
import math

import jax
import jax.numpy as jnp
from jax import lax
from jax.experimental import pallas as pl
from jax.experimental.pallas import tpu as pltpu
from jax.sharding import PartitionSpec as P

SINK_ITERS = 3
EPSILON = 0.05
SOFTMAX_TEMP_VALUE = 0.1
LOG2E = math.log2(math.e)

MESH = pl.DeviceIdType.MESH
NX, NY, NZ = 4, 4, 8
NCHIP = NY * NZ
ROWS = 1024
COLS = 1024
DIM = 1024
SHARD = 16
LANES = 128
TOTAL_ROWS = 4096
TOTAL_PROTOS = 65536
GO_STEP = 0


def swap_kernel(
    v1_ref, v2_ref, p_ref, out_ref, loss_ref,
    xg, xp, praw, pt, kern, s2, xb, vstage, squares, rscr, col_r, inv_col,
    colbuf, rowbuf, tbuf, xbuf, cvec, svec, rvec, lvec, sstat, pstat, inv_row2,
    local_sem, stage_sem, gather_rs, send_sem, xp_rs, pu_rs, col_rs, row_rs, t_rs, x_rs, vec_rs, go_sem,
):
    b = lax.axis_index("batch")
    q = lax.axis_index("proto")
    c = q % 2
    z = (q // 2) % NZ
    y = q // (2 * NZ)
    chip = y * NZ + z

    def device(bb, yy, zz, cc):
        return (bb, yy * (2 * NZ) + zz * 2 + cc)

    def at_y(d):
        return device(b, (y + d) % NY, z, c)

    def at_z(d):
        return device(b, y, (z + d) % NZ, c)

    partner = device(b, y, z, 1 - c)
    sent = []

    def remote(src, dst, rsem, dev):
        return pltpu.make_async_remote_copy(
            src_ref=src, dst_ref=dst, send_sem=send_sem, recv_sem=rsem,
            device_id=dev, device_id_type=MESH)

    def start(src, dst, rsem, dev):
        copy = remote(src, dst, rsem, dev)
        copy.start()
        sent.append(copy)

    def drain():
        for copy in sent:
            copy.wait_send()
        sent.clear()

    own_p = pltpu.make_async_copy(p_ref, praw, local_sem.at[0])
    own_p.start()

    def load(src, dst, sem):
        copy = pltpu.make_async_copy(src, dst, sem)
        copy.start()
        return copy

    barrier = pltpu.get_barrier_semaphore()
    greet = [partner]
    greet += [device((b + d) % NX, y, z, c) for d in range(1, NX)]
    greet += [at_y(d) for d in range(1, NY)]
    greet += [at_z(d) for d in range(1, NZ)]
    for dev in greet:
        pl.semaphore_signal(barrier, 1, device_id=dev, device_id_type=MESH)

    def enter():
        pl.semaphore_wait(barrier, len(greet))

    def normalize(slot):
        own_p.wait()

        def body(i, _):
            rows = pl.ds(pl.multiple_of(i * LANES, LANES), LANES)
            w = praw[rows, :].astype(jnp.float32)
            total = jnp.sum(w * w, axis=1, keepdims=True)
            unit = (w * lax.rsqrt(total + 1e-06)).astype(jnp.bfloat16)
            pt[slot, :, :, :, rows] = jnp.transpose(unit).reshape(NY, NZ, 2 * SHARD, LANES)
            return 0

        lax.fori_loop(0, COLS // LANES, body, 0)

    def put(yy, zz, h, dev):
        start(xg.at[yy, zz, h], xg.at[yy, zz, h], gather_rs.at[yy, zz, h], dev)

    def arrived(yy, zz, h):
        remote(xg.at[yy, zz, h], xg.at[yy, zz, h], gather_rs.at[yy, zz, h], partner).wait_recv()

    def hops(j, direction):
        far = NZ // 2
        if direction > 0:
            return far if j in (0, 1) else far - 1
        return far - 1 if j in (0, 1) else far

    def gather(own_half, work):
        def yj(j):
            return (y + j) % NY

        def zk(k):
            return (z + k) % NZ

        def first_puts(h):
            put(y, z, h, at_z(1))
            put(y, z, h, at_z(NZ - 1))
            for d in (2, 1, 3):
                put(y, z, h, at_y(d))

        own_half(first_puts)

        def ring(k, js):
            for direction in (1, -1):
                zz = zk(NZ - k) if direction > 0 else zk(k)
                nxt = at_z(1) if direction > 0 else at_z(NZ - 1)
                for j in js:
                    if hops(j, direction) >= k:
                        arrived(yj(j), zz, 0)
                        if hops(j, direction) > k:
                            put(yj(j), zz, 0, nxt)
                    if j == 0 and hops(1, direction) >= k:
                        arrived(y, zz, 1)
                        if hops(1, direction) > k:
                            put(y, zz, 1, nxt)
                        for d in (2, 1, 3):
                            put(y, zz, 1, at_y(d))

        far = NZ // 2
        ring(1, (0,))
        for j in (1, 3, 2):
            arrived(yj(j), z, 0)
            put(yj(j), z, 0, at_z(1))
            put(yj(j), z, 0, at_z(NZ - 1))
        for k in range(1, far + 1):
            if k < far:
                ring(k + 1, (0,))
            ring(k, (1, 3, 2))
            offsets = (k, NZ - k) if k < far else (0, far)
            if k > 1:
                work(2 * k - 3)
            for o in offsets:
                for j in (1, 3, 2):
                    arrived(yj(j), zk(o), 1)
            work(2 * k - 2, zk(offsets[0]), zk(offsets[1]))

    def row_squares(block):
        v = block.astype(jnp.float32)
        return jnp.sum((v * v).reshape(-1, 8, ROWS), axis=0)

    def spread(row, dst, g):
        dst[g * LANES:(g + 1) * LANES, :] = jnp.transpose(
            jnp.broadcast_to(row, (LANES, LANES)))

    def spread_scale(inv, factor):
        for g in range(ROWS // LANES):
            spread(inv[:, g * LANES:(g + 1) * LANES] * factor, inv_col, g)

    def inverse(sums):
        return lax.rsqrt(jnp.sum(sums, axis=0, keepdims=True) + 1e-06)

    def transpose_view(xt):
        sums = jnp.zeros((8, ROWS), jnp.float32)
        for kb in range(DIM // LANES):
            yy, z0 = kb // 2, (kb % 2) * 4
            block = xt[yy, z0:z0 + 4].reshape(LANES, ROWS)
            xb[:, kb * LANES:(kb + 1) * LANES] = jnp.transpose(block)
            sums += row_squares(block)
        return inverse(sums)

    NB = 256

    def chunk_load(k, z0, z1):
        sums = jnp.zeros((8, ROWS), jnp.float32)
        for i, zz in enumerate((z0, z1)):
            block = xg[:, zz].reshape(LANES, ROWS)
            at = (k - 1) * 2 * LANES + i * LANES
            xb[:, at:at + LANES] = jnp.transpose(block)
            sums += row_squares(block)
        if k > 1:
            sums += squares[...]
        squares[...] = sums
        if k == NZ // 2:
            spread_scale(inverse(sums), LOG2E / EPSILON)

    def chunk_product(k, z0, z1, slot):
        first, last = k == 1, k == NZ // 2
        depth = slice((k - 1) * 2 * LANES, k * 2 * LANES)
        for t in range(COLS // NB):
            lanes = slice(t * NB, (t + 1) * NB)
            rhs = jnp.concatenate([
                pt[slot, :, zz, :, lanes].reshape(LANES, NB) for zz in (z0, z1)], axis=0)
            cols = slice(slot * COLS + t * NB, slot * COLS + (t + 1) * NB)
            part = jnp.zeros((8, NB), jnp.float32)
            for m in range(ROWS // NB):
                mrows = slice(m * NB, (m + 1) * NB)
                s = jnp.dot(xb[mrows, depth], rhs, preferred_element_type=jnp.float32)
                if not first:
                    s = s + kern[mrows, cols]
                if last:
                    scale = inv_col[mrows, :]
                    s = jnp.exp2(s * jnp.concatenate([scale, scale], axis=1))
                    part += jnp.sum(s.reshape(NB // 8, 8, NB), axis=0)
                kern[mrows, cols] = s
            if last:
                total = jnp.sum(part, axis=0, keepdims=True)
                for u in range(NB // LANES):
                    row = slot * (COLS // LANES) + t * (NB // LANES) + u
                    colbuf[0, b, row:row + 1, :] = total[:, u * LANES:(u + 1) * LANES]

    MB = 512

    def products(slot, epilogue):
        def body(i, _):
            ncols = pl.ds(pl.multiple_of(i * NB, NB), NB)
            rhs = pt[slot, :, :, :, ncols].reshape(DIM, NB)
            for m in range(ROWS // MB):
                mrows = slice(m * MB, (m + 1) * MB)
                s = jnp.dot(xb[mrows, :], rhs, preferred_element_type=jnp.float32)
                epilogue(mrows, ncols, s)
            return 0

        lax.fori_loop(0, COLS // NB, body, 0)

    def kernel_block(xt, slot):
        spread_scale(transpose_view(xt), LOG2E / EPSILON)

        def epilogue(mrows, ncols, s):
            scale = inv_col[mrows, :]
            kern[mrows, ncols] = jnp.exp2(s * jnp.concatenate([scale, scale], axis=1))

        products(slot, epilogue)

    def gather_lanes(dst):
        for g in range(ROWS // LANES):
            dst[g:g + 1, :] = jnp.sum(
                jnp.transpose(rscr[g * LANES:(g + 1) * LANES, :]), axis=0, keepdims=True)

    def second_view(xt, slot):
        inv = transpose_view(xt)
        for g in range(ROWS // LANES):
            inv_row2[g:g + 1, :] = inv[:, g * LANES:(g + 1) * LANES]
        spread_scale(inv, LOG2E / SOFTMAX_TEMP_VALUE)
        rscr[...] = jnp.zeros((ROWS, LANES), jnp.float32)

        def epilogue(mrows, ncols, s):
            s2[mrows, ncols] = s
            scale = inv_col[mrows, :]
            e = jnp.exp2(s * jnp.concatenate([scale, scale], axis=1))
            rscr[mrows, :] += e[:, :LANES] + e[:, LANES:]

        products(slot, epilogue)
        gather_lanes(pstat.at[0])

    def column_pass(dst):
        nj = 2 * COLS // LANES

        def body(g, accs):
            rows = pl.ds(pl.multiple_of(g * 8, 8), 8)
            r = col_r[rows, :]
            return tuple(
                acc + kern[rows, j * LANES:(j + 1) * LANES] * r for j, acc in enumerate(accs))

        zero = jnp.zeros((8, LANES), jnp.float32)
        accs = lax.fori_loop(0, ROWS // 8, body, (zero,) * nj, unroll=4)
        for j in range(nj):
            dst[j:j + 1, :] = jnp.sum(accs[j], axis=0, keepdims=True)

    def row_pass(dst):
        nj = 2 * COLS // LANES

        def body(g, _):
            rows = pl.ds(pl.multiple_of(g * 64, 64), 64)
            acc = jnp.zeros((64, LANES), jnp.float32)
            for j in range(nj):
                acc += kern[rows, j * LANES:(j + 1) * LANES] * cvec[j:j + 1, :]
            rscr[rows, :] = acc
            return 0

        lax.fori_loop(0, ROWS // 64, body, 0, unroll=2)
        gather_lanes(dst)

    def cross_pass(k0, cref):
        def body(g, _):
            rows = pl.ds(pl.multiple_of(g * 64, 64), 64)
            acc = jnp.zeros((64, LANES), jnp.float32)
            for j in range(COLS // LANES):
                acc += (
                    kern[rows, k0 + j * LANES:k0 + (j + 1) * LANES]
                    * cref[j:j + 1, :]
                    * s2[rows, j * LANES:(j + 1) * LANES])
            rscr[rows, :] = acc
            return 0

        lax.fori_loop(0, ROWS // 64, body, 0, unroll=2)
        gather_lanes(pstat.at[1])
        pstat[1] = pstat[1] * inv_row2[...] * (1.0 / SOFTMAX_TEMP_VALUE)

    def spread_rows(rows8):
        for g in range(ROWS // LANES):
            spread(rows8[g:g + 1, :], col_r, g)

    def write_out(k0, cref):
        def body(g, _):
            rows = pl.ds(pl.multiple_of(g * LANES, LANES), LANES)
            scale = col_r[rows, :] * float(TOTAL_ROWS)
            for j in range(COLS // LANES):
                lanes = slice(j * LANES, (j + 1) * LANES)
                assign = (
                    kern[rows, k0 + j * LANES:k0 + (j + 1) * LANES] * cref[j:j + 1, :]) * scale
                out_ref[rows, lanes] = (assign * float(TOTAL_PROTOS)).astype(jnp.bfloat16)
            return 0

        lax.fori_loop(0, ROWS // LANES, body, 0)

    def exchange_columns(it):
        for d in range(1, NX):
            start(colbuf.at[it, b], colbuf.at[it, b], col_rs.at[it],
                  device((b + d) % NX, y, z, c))
        peers = colbuf.at[it, pl.ds(0, NX - 1)]
        remote(peers, peers, col_rs.at[it], partner).wait_recv()
        total = (colbuf[it, 0] + colbuf[it, 1]) + (colbuf[it, 2] + colbuf[it, 3])
        cvec[...] = 1.0 / (float(TOTAL_PROTOS) * total)

    def plane_send(ref, rsem):
        offsets = [(dy, dz) for dy in range(NY) for dz in range(NZ) if dy or dz]
        offsets.sort(key=lambda o: -(min(o[0], NY - o[0]) + min(o[1], NZ - o[1])))
        for dy, dz in offsets:
            start(ref, ref, rsem, device(b, (y + dy) % NY, (z + dz) % NZ, c))

    def plane_wait(peers, rsem):
        remote(peers, peers, rsem, partner).wait_recv()

    def share(zs):
        for zz in zs:
            start(xg.at[:, zz], xp.at[:, zz], xp_rs, partner)

    @pl.when(c == 1)
    def _():
        own = load(v1_ref, xg.at[y, z, 1], local_sem.at[1])
        other = load(v2_ref, vstage, local_sem.at[2])
        normalize(1)
        own.wait()
        other.wait()
        enter()
        start(vstage, xg.at[y, z, 1], stage_sem, partner)

        def own_half(first_puts):
            first_puts(1)
            remote(vstage, xg.at[y, z, 0], stage_sem, partner).wait_recv()
            first_puts(0)

        loaded = []

        def work(step, *zs):
            k = step // 2 + 1
            if zs:
                loaded.append(zs)
                share(zs)
                chunk_load(k, *zs)
            if step % 2 == 0:
                chunk_product(k, *loaded[k - 1], 1)
            if step == GO_STEP:
                pl.semaphore_signal(go_sem, 1, device_id=partner, device_id_type=MESH)
            if step == 1:
                remote(pt.at[0], pt.at[0], pu_rs, partner).wait_recv()
            if step % 2 == 1 or k == NZ // 2:
                chunk_product(k, *loaded[k - 1], 0)

        gather(own_half, work)
        for it in range(SINK_ITERS):
            if it > 0:
                column_pass(colbuf.at[it, b])
            exchange_columns(it)
            if it == SINK_ITERS - 1:
                start(cvec.at[pl.ds(0, 8)], svec, vec_rs.at[0], partner)
            row_pass(rowbuf.at[it, chip])
            plane_send(rowbuf.at[it, chip], row_rs.at[it])
            if it == 1:
                remote(xg, xp, xp_rs, partner).wait_recv()
                second_view(xp, 1)
                remote(pstat.at[0], sstat.at[0], vec_rs.at[4], partner).wait_recv()
                tbuf[chip] = pstat[0] + sstat[0]
                plane_send(tbuf.at[chip], t_rs)
            if it == SINK_ITERS - 1:
                cross_pass(COLS, cvec.at[pl.ds(8, 8)])
                remote(pstat.at[1], sstat.at[1], vec_rs.at[1], partner).wait_recv()
                xbuf[chip] = pstat[1] + sstat[1]
                plane_send(xbuf.at[chip], x_rs)
            plane_wait(rowbuf.at[it, pl.ds(0, NCHIP - 1)], row_rs.at[it])
            row_sums = jnp.sum(rowbuf[it], axis=0)
            rvec[...] = 1.0 / (float(TOTAL_ROWS) * row_sums)
            if it == SINK_ITERS - 1:
                start(rvec, lvec.at[0], vec_rs.at[2], partner)
            spread_rows(rvec)
        write_out(COLS, cvec.at[pl.ds(8, 8)])
        plane_wait(tbuf.at[pl.ds(0, NCHIP - 1)], t_rs)
        totals = jnp.log(jnp.sum(tbuf[...], axis=0))
        row_sums = jnp.sum(rowbuf[SINK_ITERS - 1], axis=0)
        plane_wait(xbuf.at[pl.ds(0, NCHIP - 1)], x_rs)
        loss = totals - jnp.sum(xbuf[...], axis=0) / row_sums
        loss_ref[...] = loss
        lvec[1] = loss
        start(lvec.at[1], lvec.at[1], vec_rs.at[3], partner)
        drain()

    @pl.when(c == 0)
    def _():
        own = load(v2_ref, xg.at[y, z, 0], local_sem.at[1])
        other = load(v1_ref, vstage, local_sem.at[2])
        normalize(0)
        own.wait()
        other.wait()
        enter()
        start(vstage, xg.at[y, z, 0], stage_sem, partner)
        start(pt.at[0], pt.at[0], pu_rs, partner)

        def own_half(first_puts):
            first_puts(0)
            remote(vstage, xg.at[y, z, 1], stage_sem, partner).wait_recv()
            first_puts(1)

        def work(step, *zs):
            share(zs)

        pl.semaphore_wait(go_sem, 1)
        gather(own_half, work)
        second_view(xg, 0)
        start(pstat.at[0], sstat.at[0], vec_rs.at[4], partner)
        remote(xg, xp, xp_rs, partner).wait_recv()
        kernel_block(xp, 0)
        remote(cvec.at[pl.ds(0, 8)], svec, vec_rs.at[0], partner).wait_recv()
        cross_pass(0, svec)
        start(pstat.at[1], sstat.at[1], vec_rs.at[1], partner)
        remote(rvec, lvec.at[0], vec_rs.at[2], partner).wait_recv()
        spread_rows(lvec.at[0])
        write_out(0, svec)
        remote(lvec.at[1], lvec.at[1], vec_rs.at[3], partner).wait_recv()
        loss_ref[...] = lvec[1]
        drain()


def local(view_codes, predictor_view_embeddings, prototypes):
    f32, bf16 = jnp.float32, jnp.bfloat16
    anywhere = pl.BlockSpec(memory_space=pltpu.HBM)
    vmem = pl.BlockSpec(memory_space=pltpu.VMEM)
    dma = pltpu.SemaphoreType.DMA
    assignments, loss = pl.pallas_call(
        swap_kernel,
        out_shape=(
            jax.ShapeDtypeStruct((ROWS, COLS), bf16),
            jax.ShapeDtypeStruct((8, LANES), f32),
        ),
        in_specs=[anywhere] * 3,
        out_specs=(vmem, vmem),
        scratch_shapes=[
            pltpu.VMEM((NY, NZ, 2, SHARD, ROWS), bf16),
            pltpu.VMEM((NY, NZ, 2, SHARD, ROWS), bf16),
            pltpu.VMEM((COLS, DIM), bf16),
            pltpu.VMEM((2, NY, NZ, 2 * SHARD, COLS), bf16),
            pltpu.VMEM((ROWS, 2 * COLS), f32),
            pltpu.VMEM((ROWS, COLS), f32),
            pltpu.VMEM((ROWS, DIM), bf16),
            pltpu.VMEM((SHARD, ROWS), bf16),
            pltpu.VMEM((8, ROWS), f32),
            pltpu.VMEM((ROWS, LANES), f32),
            pltpu.VMEM((ROWS, LANES), f32),
            pltpu.VMEM((ROWS, LANES), f32),
            pltpu.VMEM((SINK_ITERS, NX, 16, LANES), f32),
            pltpu.VMEM((SINK_ITERS, NCHIP, 8, LANES), f32),
            pltpu.VMEM((NCHIP, 8, LANES), f32),
            pltpu.VMEM((NCHIP, 8, LANES), f32),
            pltpu.VMEM((16, LANES), f32),
            pltpu.VMEM((8, LANES), f32),
            pltpu.VMEM((8, LANES), f32),
            pltpu.VMEM((2, 8, LANES), f32),
            pltpu.VMEM((2, 8, LANES), f32),
            pltpu.VMEM((2, 8, LANES), f32),
            pltpu.VMEM((8, LANES), f32),
            dma((3,)),
            dma(()),
            dma((NY, NZ, 2)),
            dma(()),
            dma(()),
            dma(()),
            dma((SINK_ITERS,)),
            dma((SINK_ITERS,)),
            dma(()),
            dma(()),
            dma((5,)),
            pltpu.SemaphoreType.REGULAR,
        ],
        compiler_params=pltpu.CompilerParams(
            collective_id=0, has_side_effects=True, vmem_limit_bytes=48 << 20),
        name="swapped_sinkhorn",
    )(*[pltpu.with_memory_space_constraint(a, pltpu.HBM) for a in (
        view_codes.T, predictor_view_embeddings.T, prototypes)])
    return assignments, loss.reshape(ROWS)


def solution(mesh):
    placed = (P("batch", "proto"), P("batch", "proto"), P("proto", None))
    return jax.shard_map(
        local,
        mesh=mesh,
        in_specs=placed,
        out_specs=(P("batch", "proto"), P("batch")),
        check_vma=False,
    )
```

time: 82.1 us -> 64.7 us (0.79)
  Pallas kernels: 76.2 us -> 62.1 us
  local copies, waits for them, and re-layouts: 5.01 us -> 1.91 us
    pallas_call x1, Pallas kernels: 76.2 us -> 62.1 us  [local(): pl.pallas_call(swap_kernel, out_shape=(jax.ShapeDtypeStruct((ROWS, COLS),...]
    unnamed x8 -> x2, local copies, waits for them, and re-layouts: 5.01 us -> 1.91 us
where the time goes in v2:
time: 64.7 us; the launch traced here: 64.6 us
  Pallas kernels  62.1 us (96%)
  local copies, waits for them, and re-layouts  1.91 us (3%)
    pallas_call x1, Pallas kernels, local(): pl.pallas_call(swap_kernel, out_shape=(jax.ShapeDtypeStruct((ROWS, COLS),...  62.1 us
    unnamed x2, local copies, waits for them, and re-layouts  1.91 us

profile of v2, /device:TPU:1, one launch (start us, length us, event | category | flops | bytes accessed | tf_op | source)
XLA Modules:
  0.0 64.6 jit_solution(10319995132301757729)
XLA Ops:
  0.6 62.1 %swapped_sinkhorn.1 = (bf16[1024,1024]{1,0:T(8,128)(2,1)S(1)}, f32[8,128]{1,0:T(8,128)S(1)}) custom-call(bf16[16,1024]{1,0:T(8,128)(2,1)} %bitcast.4, bf16[16,1024]{1,0:T(8,128)(2,1)} %bitcast.5, bf16[1024,1024]{1,0:T(8,128)(2,1)} %p_ref.1), custom_call_target="tpu_custom_call" | custom-call | tf_op jit(solution)/shard_map/swapped_sinkhorn/pallas_call | solution.py:463
  62.7 1.3 %copy.7 = bf16[1024,1024]{1,0:T(8,128)(2,1)} copy(bf16[1024,1024]{1,0:T(8,128)(2,1)S(1)} %get-tuple-element.8) | data formatting | bytes 4194304
  64.0 0.6 copy.8

commit v3 on v2

--- a/solution.py
+++ b/solution.py
@@ -23,14 +23,13 @@
 LANES = 128
 TOTAL_ROWS = 4096
 TOTAL_PROTOS = 65536
-GO_STEP = 0
 
 
 def swap_kernel(
     v1_ref, v2_ref, p_ref, out_ref, loss_ref,
     xg, xp, praw, pt, kern, s2, xb, vstage, squares, rscr, col_r, inv_col,
     colbuf, rowbuf, tbuf, xbuf, cvec, svec, rvec, lvec, sstat, pstat, inv_row2,
-    local_sem, stage_sem, gather_rs, send_sem, xp_rs, pu_rs, col_rs, row_rs, t_rs, x_rs, vec_rs, go_sem,
+    local_sem, gather_rs, send_sem, xp_rs, pu_rs, col_rs, row_rs, t_rs, x_rs, vec_rs, go_sem,
 ):
     b = lax.axis_index("batch")
     q = lax.axis_index("proto")
@@ -77,8 +76,9 @@
     barrier = pltpu.get_barrier_semaphore()
     greet = [partner]
     greet += [device((b + d) % NX, y, z, c) for d in range(1, NX)]
-    greet += [at_y(d) for d in range(1, NY)]
-    greet += [at_z(d) for d in range(1, NZ)]
+    near = [(d, 0) for d in (2, 1, 3)] + [(0, 1), (0, NZ - 1)]
+    for cc in (c, 1 - c):
+        greet += [device(b, (y + dy) % NY, (z + dz) % NZ, cc) for dy, dz in near]
     for dev in greet:
         pl.semaphore_signal(barrier, 1, device_id=dev, device_id_type=MESH)
 
@@ -110,20 +110,25 @@
             return far if j in (0, 1) else far - 1
         return far - 1 if j in (0, 1) else far
 
-    def gather(own_half, work):
+    def hand_over(h):
+        opposite = 1 - c
+        rsem = gather_rs.at[y, z, h]
+        for dy, dz in ((0, 1), (0, NZ - 1), (2, 0), (1, 0), (3, 0)):
+            start(vstage, xg.at[y, z, h], rsem,
+                  device(b, (y + dy) % NY, (z + dz) % NZ, opposite))
+        start(vstage, xg.at[y, z, h], rsem, partner)
+
+    def gather(own, work):
         def yj(j):
             return (y + j) % NY
 
         def zk(k):
             return (z + k) % NZ
 
-        def first_puts(h):
-            put(y, z, h, at_z(1))
-            put(y, z, h, at_z(NZ - 1))
-            for d in (2, 1, 3):
-                put(y, z, h, at_y(d))
-
-        own_half(first_puts)
+        put(y, z, own, at_z(1))
+        put(y, z, own, at_z(NZ - 1))
+        for d in (2, 1, 3):
+            put(y, z, own, at_y(d))
 
         def ring(k, js):
             for direction in (1, -1):
@@ -150,14 +155,16 @@
         for k in range(1, far + 1):
             if k < far:
                 ring(k + 1, (0,))
+                if k > 1:
+                    work(k - 1)
             ring(k, (1, 3, 2))
             offsets = (k, NZ - k) if k < far else (0, far)
-            if k > 1:
-                work(2 * k - 3)
             for o in offsets:
                 for j in (1, 3, 2):
                     arrived(yj(j), zk(o), 1)
-            work(2 * k - 2, zk(offsets[0]), zk(offsets[1]))
+            if k == far:
+                arrived(y, z, 1 - own)
+            work(k, zk(offsets[0]), zk(offsets[1]))
 
     def row_squares(block):
         v = block.astype(jnp.float32)
@@ -242,7 +249,9 @@
 
         def epilogue(mrows, ncols, s):
             scale = inv_col[mrows, :]
-            kern[mrows, ncols] = jnp.exp2(s * jnp.concatenate([scale, scale], axis=1))
+            value = jnp.exp2(s * jnp.concatenate([scale, scale], axis=1))
+            kern[mrows, ncols] = value
+            s2[mrows, ncols] = s2[mrows, ncols] * value
 
         products(slot, epilogue)
 
@@ -295,15 +304,15 @@
         lax.fori_loop(0, ROWS // 64, body, 0, unroll=2)
         gather_lanes(dst)
 
-    def cross_pass(k0, cref):
+    def cross_pass(k0, cref, ready):
         def body(g, _):
             rows = pl.ds(pl.multiple_of(g * 64, 64), 64)
             acc = jnp.zeros((64, LANES), jnp.float32)
             for j in range(COLS // LANES):
-                acc += (
-                    kern[rows, k0 + j * LANES:k0 + (j + 1) * LANES]
-                    * cref[j:j + 1, :]
-                    * s2[rows, j * LANES:(j + 1) * LANES])
+                term = s2[rows, j * LANES:(j + 1) * LANES] * cref[j:j + 1, :]
+                if not ready:
+                    term = term * kern[rows, k0 + j * LANES:k0 + (j + 1) * LANES]
+                acc += term
             rscr[rows, :] = acc
             return 0
 
@@ -358,31 +367,25 @@
         own.wait()
         other.wait()
         enter()
-        start(vstage, xg.at[y, z, 1], stage_sem, partner)
-
-        def own_half(first_puts):
-            first_puts(1)
-            remote(vstage, xg.at[y, z, 0], stage_sem, partner).wait_recv()
-            first_puts(0)
-
-        loaded = []
-
-        def work(step, *zs):
-            k = step // 2 + 1
-            if zs:
-                loaded.append(zs)
-                share(zs)
-                chunk_load(k, *zs)
-            if step % 2 == 0:
-                chunk_product(k, *loaded[k - 1], 1)
-            if step == GO_STEP:
+        hand_over(1)
+        far = NZ // 2
+        loaded = [None]
+
+        def work(k, *zs):
+            if not zs:
+                chunk_product(k, *loaded[k], 0)
+                return
+            loaded.append(zs)
+            share(zs)
+            chunk_load(k, *zs)
+            chunk_product(k, *zs, 1)
+            if k == 1:
                 pl.semaphore_signal(go_sem, 1, device_id=partner, device_id_type=MESH)
-            if step == 1:
                 remote(pt.at[0], pt.at[0], pu_rs, partner).wait_recv()
-            if step % 2 == 1 or k == NZ // 2:
-                chunk_product(k, *loaded[k - 1], 0)
-
-        gather(own_half, work)
+            if k >= far - 1:
+                chunk_product(k, *zs, 0)
+
+        gather(1, work)
         for it in range(SINK_ITERS):
             if it > 0:
                 column_pass(colbuf.at[it, b])
@@ -398,7 +401,7 @@
                 tbuf[chip] = pstat[0] + sstat[0]
                 plane_send(tbuf.at[chip], t_rs)
             if it == SINK_ITERS - 1:
-                cross_pass(COLS, cvec.at[pl.ds(8, 8)])
+                cross_pass(COLS, cvec.at[pl.ds(8, 8)], False)
                 remote(pstat.at[1], sstat.at[1], vec_rs.at[1], partner).wait_recv()
                 xbuf[chip] = pstat[1] + sstat[1]
                 plane_send(xbuf.at[chip], x_rs)
@@ -427,25 +430,16 @@
         own.wait()
         other.wait()
         enter()
-        start(vstage, xg.at[y, z, 0], stage_sem, partner)
+        hand_over(0)
         start(pt.at[0], pt.at[0], pu_rs, partner)
-
-        def own_half(first_puts):
-            first_puts(0)
-            remote(vstage, xg.at[y, z, 1], stage_sem, partner).wait_recv()
-            first_puts(1)
-
-        def work(step, *zs):
-            share(zs)
-
         pl.semaphore_wait(go_sem, 1)
-        gather(own_half, work)
+        gather(0, lambda k, *zs: share(zs))
         second_view(xg, 0)
         start(pstat.at[0], sstat.at[0], vec_rs.at[4], partner)
         remote(xg, xp, xp_rs, partner).wait_recv()
         kernel_block(xp, 0)
         remote(cvec.at[pl.ds(0, 8)], svec, vec_rs.at[0], partner).wait_recv()
-        cross_pass(0, svec)
+        cross_pass(0, svec, True)
         start(pstat.at[1], sstat.at[1], vec_rs.at[1], partner)
         remote(rvec, lvec.at[0], vec_rs.at[2], partner).wait_recv()
         spread_rows(lvec.at[0])
@@ -493,7 +487,6 @@
             pltpu.VMEM((2, 8, LANES), f32),
             pltpu.VMEM((8, LANES), f32),
             dma((3,)),
-            dma(()),
             dma((NY, NZ, 2)),
             dma(()),
             dma(()),

time: 64.7 us -> 63.3 us (0.978)
  Pallas kernels: 62.1 us -> 60.6 us
    pallas_call x1, Pallas kernels: 62.1 us -> 60.6 us  [local(): pl.pallas_call(swap_kernel, out_shape=(jax.ShapeDtypeStruct((ROWS, COLS),...]
where the time goes in v3:
time: 63.3 us; the launch traced here: 63.2 us
  Pallas kernels  60.6 us (96%)
  local copies, waits for them, and re-layouts  1.91 us (3%)
  between operations  0.64 us (1%)
    pallas_call x1, Pallas kernels, local(): pl.pallas_call(swap_kernel, out_shape=(jax.ShapeDtypeStruct((ROWS, COLS),...  60.6 us
    unnamed x2, local copies, waits for them, and re-layouts  1.91 us

profile of v3, /device:TPU:1, one launch (start us, length us, event | category | flops | bytes accessed | tf_op | source)
XLA Modules:
  0.0 63.2 jit_solution(17811438274108130801)
XLA Ops:
  0.6 60.6 %swapped_sinkhorn.1 = (bf16[1024,1024]{1,0:T(8,128)(2,1)S(1)}, f32[8,128]{1,0:T(8,128)S(1)}) custom-call(bf16[16,1024]{1,0:T(8,128)(2,1)} %bitcast.4, bf16[16,1024]{1,0:T(8,128)(2,1)} %bitcast.5, bf16[1024,1024]{1,0:T(8,128)(2,1)} %p_ref.1), custom_call_target="tpu_custom_call" | custom-call | tf_op jit(solution)/shard_map/swapped_sinkhorn/pallas_call | solution.py:457
  61.3 1.3 %copy.7 = bf16[1024,1024]{1,0:T(8,128)(2,1)} copy(bf16[1024,1024]{1,0:T(8,128)(2,1)S(1)} %get-tuple-element.8) | data formatting | bytes 4194304
  62.6 0.6 copy.8

commit v4 on v3

--- a/solution.py
+++ b/solution.py
@@ -23,12 +23,13 @@
 LANES = 128
 TOTAL_ROWS = 4096
 TOTAL_PROTOS = 65536
+GO_AT = 2
 
 
 def swap_kernel(
     v1_ref, v2_ref, p_ref, out_ref, loss_ref,
     xg, xp, praw, pt, kern, s2, xb, vstage, squares, rscr, col_r, inv_col,
-    colbuf, rowbuf, tbuf, xbuf, cvec, svec, rvec, lvec, sstat, pstat, inv_row2,
+    colacc, rsum, colbuf, rowbuf, tbuf, xbuf, cvec, svec, rvec, lvec, sstat, pstat, inv_row2,
     local_sem, gather_rs, send_sem, xp_rs, pu_rs, col_rs, row_rs, t_rs, x_rs, vec_rs, go_sem,
 ):
     b = lax.axis_index("batch")
@@ -66,7 +67,6 @@
         sent.clear()
 
     own_p = pltpu.make_async_copy(p_ref, praw, local_sem.at[0])
-    own_p.start()
 
     def load(src, dst, sem):
         copy = pltpu.make_async_copy(src, dst, sem)
@@ -76,7 +76,7 @@
     barrier = pltpu.get_barrier_semaphore()
     greet = [partner]
     greet += [device((b + d) % NX, y, z, c) for d in range(1, NX)]
-    near = [(d, 0) for d in (2, 1, 3)] + [(0, 1), (0, NZ - 1)]
+    near = [(d, 0) for d in (2, 1, 3)] + [(0, d) for d in (1, NZ - 1)]
     for cc in (c, 1 - c):
         greet += [device(b, (y + dy) % NY, (z + dz) % NZ, cc) for dy, dz in near]
     for dev in greet:
@@ -110,61 +110,76 @@
             return far if j in (0, 1) else far - 1
         return far - 1 if j in (0, 1) else far
 
-    def hand_over(h):
-        opposite = 1 - c
+    def targets(h, steps):
+        along_z = [(0, sign * st) for st in steps for sign in (1, -1)]
+        along_y = [(2, 0), (1, 0), (3, 0)]
+        return along_y + along_z if h == 0 else along_z + along_y
+
+    def hand_over(h, steps):
         rsem = gather_rs.at[y, z, h]
-        for dy, dz in ((0, 1), (0, NZ - 1), (2, 0), (1, 0), (3, 0)):
+        for dy, dz in targets(h, steps):
             start(vstage, xg.at[y, z, h], rsem,
-                  device(b, (y + dy) % NY, (z + dz) % NZ, opposite))
+                  device(b, (y + dy) % NY, (z + dz + NZ) % NZ, 1 - c))
         start(vstage, xg.at[y, z, h], rsem, partner)
 
-    def gather(own, work):
-        def yj(j):
-            return (y + j) % NY
-
-        def zk(k):
-            return (z + k) % NZ
-
-        put(y, z, own, at_z(1))
-        put(y, z, own, at_z(NZ - 1))
-        for d in (2, 1, 3):
-            put(y, z, own, at_y(d))
-
-        def ring(k, js):
-            for direction in (1, -1):
-                zz = zk(NZ - k) if direction > 0 else zk(k)
-                nxt = at_z(1) if direction > 0 else at_z(NZ - 1)
-                for j in js:
-                    if hops(j, direction) >= k:
-                        arrived(yj(j), zz, 0)
-                        if hops(j, direction) > k:
-                            put(yj(j), zz, 0, nxt)
-                    if j == 0 and hops(1, direction) >= k:
-                        arrived(y, zz, 1)
-                        if hops(1, direction) > k:
-                            put(y, zz, 1, nxt)
+    def first_puts(h, steps):
+        for dy, dz in targets(h, steps):
+            put(y, z, h, device(b, (y + dy) % NY, (z + dz + NZ) % NZ, c))
+
+    def yj(j):
+        return (y + j) % NY
+
+    def zk(k):
+        return (z + k + NZ) % NZ
+
+    def ring(k, js, children):
+        for direction in (1, -1):
+            zz = zk(-direction * k)
+            for j in js:
+                for h in ((0, 1) if j == 0 else (0,)):
+                    reach = hops(1 if h else j, direction)
+                    if reach < k:
+                        continue
+                    arrived(yj(j), zz, h)
+                    for st in children.get(k, ()):
+                        if k + st <= reach:
+                            put(yj(j), zz, h, at_z(zk(direction * st) - z + NZ))
+                    if h:
                         for d in (2, 1, 3):
                             put(y, zz, 1, at_y(d))
 
+    def local_units(steps):
+        for i, st in enumerate(steps):
+            for j in (1, 3, 2):
+                if i == 0:
+                    arrived(yj(j), z, 0)
+                put(yj(j), z, 0, at_z(st))
+                put(yj(j), z, 0, at_z(NZ - st))
+
+    def finish(k, own, work):
         far = NZ // 2
-        ring(1, (0,))
-        for j in (1, 3, 2):
-            arrived(yj(j), z, 0)
-            put(yj(j), z, 0, at_z(1))
-            put(yj(j), z, 0, at_z(NZ - 1))
+        offsets = (k, NZ - k) if k < far else (0, far)
+        for o in offsets:
+            for j in (1, 3, 2):
+                arrived(yj(j), zk(o), 1)
+        if k == far:
+            arrived(y, z, 1 - own)
+        work(k, zk(offsets[0]), zk(offsets[1]))
+
+    def gather(own, work, go):
+        far = NZ // 2
+        children = {k: (1,) for k in range(far)}
+        ring(1, (0,), children)
+        local_units((1,))
         for k in range(1, far + 1):
             if k < far:
-                ring(k + 1, (0,))
+                ring(k + 1, (0,), children)
                 if k > 1:
                     work(k - 1)
-            ring(k, (1, 3, 2))
-            offsets = (k, NZ - k) if k < far else (0, far)
-            for o in offsets:
-                for j in (1, 3, 2):
-                    arrived(yj(j), zk(o), 1)
-            if k == far:
-                arrived(y, z, 1 - own)
-            work(k, zk(offsets[0]), zk(offsets[1]))
+            ring(k, (1, 3, 2), children)
+            if k == GO_AT:
+                go()
+            finish(k, own, work)
 
     def row_squares(block):
         v = block.astype(jnp.float32)
@@ -227,8 +242,8 @@
             if last:
                 total = jnp.sum(part, axis=0, keepdims=True)
                 for u in range(NB // LANES):
-                    row = slot * (COLS // LANES) + t * (NB // LANES) + u
-                    colbuf[0, b, row:row + 1, :] = total[:, u * LANES:(u + 1) * LANES]
+                    row = t * (NB // LANES) + u
+                    colbuf[0, slot, b, row:row + 1, :] = total[:, u * LANES:(u + 1) * LANES]
 
     MB = 512
 
@@ -255,10 +270,11 @@
 
         products(slot, epilogue)
 
-    def gather_lanes(dst):
-        for g in range(ROWS // LANES):
+    def gather_lanes(dst, first=0, count=ROWS // LANES):
+        for g in range(count):
+            at = (first + g) * LANES
             dst[g:g + 1, :] = jnp.sum(
-                jnp.transpose(rscr[g * LANES:(g + 1) * LANES, :]), axis=0, keepdims=True)
+                jnp.transpose(rscr[at:at + LANES, :]), axis=0, keepdims=True)
 
     def second_view(xt, slot):
         inv = transpose_view(xt)
@@ -276,33 +292,40 @@
         products(slot, epilogue)
         gather_lanes(pstat.at[0])
 
-    def column_pass(dst):
-        nj = 2 * COLS // LANES
-
+    nj = COLS // LANES
+    half_groups = ROWS // 16
+
+    def column_sums(cols, g0, init):
         def body(g, accs):
             rows = pl.ds(pl.multiple_of(g * 8, 8), 8)
             r = col_r[rows, :]
             return tuple(
-                acc + kern[rows, j * LANES:(j + 1) * LANES] * r for j, acc in enumerate(accs))
-
+                acc + kern[rows, j * LANES:(j + 1) * LANES] * r for j, acc in zip(cols, accs))
+
+        return lax.fori_loop(g0, g0 + half_groups, body, init, unroll=4)
+
+    def columns_a():
+        cols = range(2 * nj)
         zero = jnp.zeros((8, LANES), jnp.float32)
-        accs = lax.fori_loop(0, ROWS // 8, body, (zero,) * nj, unroll=4)
-        for j in range(nj):
-            dst[j:j + 1, :] = jnp.sum(accs[j], axis=0, keepdims=True)
-
-    def row_pass(dst):
-        nj = 2 * COLS // LANES
-
+        for j, acc in zip(cols, column_sums(cols, 0, (zero,) * (2 * nj))):
+            colacc[j] = acc
+
+    def columns_b(it, slot):
+        cols = range(slot * nj, (slot + 1) * nj)
+        accs = column_sums(cols, half_groups, tuple(colacc[j] for j in cols))
+        for j, acc in enumerate(accs):
+            colbuf[it, slot, b, j:j + 1, :] = jnp.sum(acc, axis=0, keepdims=True)
+
+    def rows_slot(slot, r0, count):
         def body(g, _):
-            rows = pl.ds(pl.multiple_of(g * 64, 64), 64)
-            acc = jnp.zeros((64, LANES), jnp.float32)
-            for j in range(nj):
+            rows = pl.ds(pl.multiple_of(r0 + g * 64, 64), 64)
+            acc = rscr[rows, :] if slot else jnp.zeros((64, LANES), jnp.float32)
+            for j in range(slot * nj, (slot + 1) * nj):
                 acc += kern[rows, j * LANES:(j + 1) * LANES] * cvec[j:j + 1, :]
             rscr[rows, :] = acc
             return 0
 
-        lax.fori_loop(0, ROWS // 64, body, 0, unroll=2)
-        gather_lanes(dst)
+        lax.fori_loop(0, count // 64, body, 0, unroll=2)
 
     def cross_pass(k0, cref, ready):
         def body(g, _):
@@ -324,27 +347,38 @@
         for g in range(ROWS // LANES):
             spread(rows8[g:g + 1, :], col_r, g)
 
-    def write_out(k0, cref):
+    def weigh(k0, cref):
         def body(g, _):
-            rows = pl.ds(pl.multiple_of(g * LANES, LANES), LANES)
-            scale = col_r[rows, :] * float(TOTAL_ROWS)
+            rows = pl.ds(pl.multiple_of(g * 64, 64), 64)
             for j in range(COLS // LANES):
-                lanes = slice(j * LANES, (j + 1) * LANES)
-                assign = (
-                    kern[rows, k0 + j * LANES:k0 + (j + 1) * LANES] * cref[j:j + 1, :]) * scale
-                out_ref[rows, lanes] = (assign * float(TOTAL_PROTOS)).astype(jnp.bfloat16)
+                lanes = slice(k0 + j * LANES, k0 + (j + 1) * LANES)
+                kern[rows, lanes] = kern[rows, lanes] * cref[j:j + 1, :]
             return 0
 
-        lax.fori_loop(0, ROWS // LANES, body, 0)
-
-    def exchange_columns(it):
-        for d in range(1, NX):
-            start(colbuf.at[it, b], colbuf.at[it, b], col_rs.at[it],
+        lax.fori_loop(0, ROWS // 64, body, 0)
+
+    def write_out(k0):
+        def body(g, _):
+            rows = pl.ds(pl.multiple_of(g * 64, 64), 64)
+            scale = col_r[rows, :] * float(TOTAL_ROWS * TOTAL_PROTOS)
+            for j in range(COLS // LANES):
+                out_ref[rows, j * LANES:(j + 1) * LANES] = (
+                    kern[rows, k0 + j * LANES:k0 + (j + 1) * LANES] * scale).astype(jnp.bfloat16)
+            return 0
+
+        lax.fori_loop(0, ROWS // 64, body, 0, unroll=2)
+
+    def send_columns(it, slot):
+        for d in (2, 1, 3):
+            start(colbuf.at[it, slot, b], colbuf.at[it, slot, b], col_rs.at[it, slot],
                   device((b + d) % NX, y, z, c))
-        peers = colbuf.at[it, pl.ds(0, NX - 1)]
-        remote(peers, peers, col_rs.at[it], partner).wait_recv()
-        total = (colbuf[it, 0] + colbuf[it, 1]) + (colbuf[it, 2] + colbuf[it, 3])
-        cvec[...] = 1.0 / (float(TOTAL_PROTOS) * total)
+
+    def wait_columns(it, slot):
+        peers = colbuf.at[it, slot, pl.ds(0, NX - 1)]
+        remote(peers, peers, col_rs.at[it, slot], partner).wait_recv()
+        total = (colbuf[it, slot, 0] + colbuf[it, slot, 1]) + (
+            colbuf[it, slot, 2] + colbuf[it, slot, 3])
+        cvec[slot * nj:(slot + 1) * nj, :] = 1.0 / (float(TOTAL_PROTOS) * total)
 
     def plane_send(ref, rsem):
         offsets = [(dy, dz) for dy in range(NY) for dz in range(NZ) if dy or dz]
@@ -363,37 +397,50 @@
     def _():
         own = load(v1_ref, xg.at[y, z, 1], local_sem.at[1])
         other = load(v2_ref, vstage, local_sem.at[2])
-        normalize(1)
+        own_p.start()
         own.wait()
         other.wait()
         enter()
-        hand_over(1)
-        far = NZ // 2
+        first_puts(1, (1,))
+        hand_over(1, (1,))
+        normalize(1)
+
+        def go():
+            pl.semaphore_signal(go_sem, 1, device_id=partner, device_id_type=MESH)
+
         loaded = [None]
 
         def work(k, *zs):
             if not zs:
+                if k == 1:
+                    remote(pt.at[0], pt.at[0], pu_rs, partner).wait_recv()
                 chunk_product(k, *loaded[k], 0)
                 return
             loaded.append(zs)
             share(zs)
             chunk_load(k, *zs)
-            chunk_product(k, *zs, 1)
-            if k == 1:
-                pl.semaphore_signal(go_sem, 1, device_id=partner, device_id_type=MESH)
-                remote(pt.at[0], pt.at[0], pu_rs, partner).wait_recv()
-            if k >= far - 1:
-                chunk_product(k, *zs, 0)
-
-        gather(1, work)
+            for slot in (1, 0) if k >= NZ // 2 - 1 else (1,):
+                chunk_product(k, *zs, slot)
+                if k == NZ // 2:
+                    send_columns(0, slot)
+
+        gather(1, work, go)
+        last = SINK_ITERS - 1
         for it in range(SINK_ITERS):
             if it > 0:
-                column_pass(colbuf.at[it, b])
-            exchange_columns(it)
-            if it == SINK_ITERS - 1:
+                columns_b(it, 0)
+                send_columns(it, 0)
+                columns_b(it, 1)
+                send_columns(it, 1)
+            wait_columns(it, 0)
+            if it == last:
                 start(cvec.at[pl.ds(0, 8)], svec, vec_rs.at[0], partner)
-            row_pass(rowbuf.at[it, chip])
-            plane_send(rowbuf.at[it, chip], row_rs.at[it])
+            rows_slot(0, 0, ROWS)
+            wait_columns(it, 1)
+            for half in range(2):
+                rows_slot(1, half * (ROWS // 2), ROWS // 2)
+                gather_lanes(rowbuf.at[it, half, chip], half * 4, 4)
+                plane_send(rowbuf.at[it, half, chip], row_rs.at[it, half])
             if it == 1:
                 remote(xg, xp, xp_rs, partner).wait_recv()
                 second_view(xp, 1)
@@ -405,18 +452,23 @@
                 remote(pstat.at[1], sstat.at[1], vec_rs.at[1], partner).wait_recv()
                 xbuf[chip] = pstat[1] + sstat[1]
                 plane_send(xbuf.at[chip], x_rs)
-            plane_wait(rowbuf.at[it, pl.ds(0, NCHIP - 1)], row_rs.at[it])
-            row_sums = jnp.sum(rowbuf[it], axis=0)
-            rvec[...] = 1.0 / (float(TOTAL_ROWS) * row_sums)
-            if it == SINK_ITERS - 1:
-                start(rvec, lvec.at[0], vec_rs.at[2], partner)
-            spread_rows(rvec)
-        write_out(COLS, cvec.at[pl.ds(8, 8)])
+                weigh(COLS, cvec.at[pl.ds(8, 8)])
+            for half in range(2):
+                plane_wait(rowbuf.at[it, half, pl.ds(0, NCHIP - 1)], row_rs.at[it, half])
+                sums = jnp.sum(rowbuf[it, half], axis=0)
+                rsum[half * 4:half * 4 + 4, :] = sums
+                rvec[half * 4:half * 4 + 4, :] = 1.0 / (float(TOTAL_ROWS) * sums)
+                if it == last and half:
+                    start(rvec, lvec.at[0], vec_rs.at[2], partner)
+                for g in range(half * 4, half * 4 + 4):
+                    spread(rvec[g:g + 1, :], col_r, g)
+                if it < last and not half:
+                    columns_a()
+        write_out(COLS)
         plane_wait(tbuf.at[pl.ds(0, NCHIP - 1)], t_rs)
         totals = jnp.log(jnp.sum(tbuf[...], axis=0))
-        row_sums = jnp.sum(rowbuf[SINK_ITERS - 1], axis=0)
         plane_wait(xbuf.at[pl.ds(0, NCHIP - 1)], x_rs)
-        loss = totals - jnp.sum(xbuf[...], axis=0) / row_sums
+        loss = totals - jnp.sum(xbuf[...], axis=0) / rsum[...]
         loss_ref[...] = loss
         lvec[1] = loss
         start(lvec.at[1], lvec.at[1], vec_rs.at[3], partner)
@@ -426,14 +478,16 @@
     def _():
         own = load(v2_ref, xg.at[y, z, 0], local_sem.at[1])
         other = load(v1_ref, vstage, local_sem.at[2])
-        normalize(0)
+        own_p.start()
         own.wait()
         other.wait()
         enter()
-        hand_over(0)
+        hand_over(0, (1,))
+        normalize(0)
         start(pt.at[0], pt.at[0], pu_rs, partner)
         pl.semaphore_wait(go_sem, 1)
-        gather(0, lambda k, *zs: share(zs))
+        first_puts(0, (1,))
+        gather(0, lambda k, *zs: share(zs), lambda: None)
         second_view(xg, 0)
         start(pstat.at[0], sstat.at[0], vec_rs.at[4], partner)
         remote(xg, xp, xp_rs, partner).wait_recv()
@@ -441,9 +495,10 @@
         remote(cvec.at[pl.ds(0, 8)], svec, vec_rs.at[0], partner).wait_recv()
         cross_pass(0, svec, True)
         start(pstat.at[1], sstat.at[1], vec_rs.at[1], partner)
+        weigh(0, svec)
         remote(rvec, lvec.at[0], vec_rs.at[2], partner).wait_recv()
         spread_rows(lvec.at[0])
-        write_out(0, svec)
+        write_out(0)
         remote(lvec.at[1], lvec.at[1], vec_rs.at[3], partner).wait_recv()
         loss_ref[...] = lvec[1]
         drain()
@@ -475,8 +530,10 @@
             pltpu.VMEM((ROWS, LANES), f32),
             pltpu.VMEM((ROWS, LANES), f32),
             pltpu.VMEM((ROWS, LANES), f32),
-            pltpu.VMEM((SINK_ITERS, NX, 16, LANES), f32),
-            pltpu.VMEM((SINK_ITERS, NCHIP, 8, LANES), f32),
+            pltpu.VMEM((16, 8, LANES), f32),
+            pltpu.VMEM((8, LANES), f32),
+            pltpu.VMEM((SINK_ITERS, 2, NX, 8, LANES), f32),
+            pltpu.VMEM((SINK_ITERS, 2, NCHIP, 4, LANES), f32),
             pltpu.VMEM((NCHIP, 8, LANES), f32),
             pltpu.VMEM((NCHIP, 8, LANES), f32),
             pltpu.VMEM((16, LANES), f32),
@@ -491,8 +548,8 @@
             dma(()),
             dma(()),
             dma(()),
-            dma((SINK_ITERS,)),
-            dma((SINK_ITERS,)),
+            dma((SINK_ITERS, 2)),
+            dma((SINK_ITERS, 2)),
             dma(()),
             dma(()),
             dma((5,)),

time: 63.3 us -> 61.3 us (0.968)
  Pallas kernels: 60.6 us -> 58.7 us
    pallas_call x1, Pallas kernels: 60.6 us -> 58.7 us  [local(): pl.pallas_call(swap_kernel, out_shape=(jax.ShapeDtypeStruct((ROWS, COLS),...]
where the time goes in v4:
time: 61.3 us; the launch traced here: 61.2 us
  Pallas kernels  58.7 us (96%)
  local copies, waits for them, and re-layouts  1.91 us (3%)
  between operations  0.64 us (1%)
    pallas_call x1, Pallas kernels, local(): pl.pallas_call(swap_kernel, out_shape=(jax.ShapeDtypeStruct((ROWS, COLS),...  58.7 us
    unnamed x2, local copies, waits for them, and re-layouts  1.91 us

profile of v4, /device:TPU:1, one launch (start us, length us, event | category | flops | bytes accessed | tf_op | source)
XLA Modules:
  0.0 61.2 jit_solution(10033532572810313511)
XLA Ops:
  0.6 58.7 %swapped_sinkhorn.1 = (bf16[1024,1024]{1,0:T(8,128)(2,1)S(1)}, f32[8,128]{1,0:T(8,128)S(1)}) custom-call(bf16[16,1024]{1,0:T(8,128)(2,1)} %bitcast.4, bf16[16,1024]{1,0:T(8,128)(2,1)} %bitcast.5, bf16[1024,1024]{1,0:T(8,128)(2,1)} %p_ref.1), custom_call_target="tpu_custom_call" | custom-call | tf_op jit(solution)/shard_map/swapped_sinkhorn/pallas_call | solution.py:512
  59.3 1.3 %copy.7 = bf16[1024,1024]{1,0:T(8,128)(2,1)} copy(bf16[1024,1024]{1,0:T(8,128)(2,1)S(1)} %get-tuple-element.8) | data formatting | bytes 4194304
  60.6 0.6 copy.8

commit v5 on v4

--- a/solution.py
+++ b/solution.py
@@ -159,10 +159,11 @@
     def finish(k, own, work):
         far = NZ // 2
         offsets = (k, NZ - k) if k < far else (0, far)
-        for o in offsets:
+        ready = {far - 1: offsets + (0,), far: (far,)}.get(k, offsets)
+        for o in ready:
             for j in (1, 3, 2):
                 arrived(yj(j), zk(o), 1)
-        if k == far:
+        if k == far - 1:
             arrived(y, z, 1 - own)
         work(k, zk(offsets[0]), zk(offsets[1]))
 
@@ -207,9 +208,9 @@
 
     NB = 256
 
-    def chunk_load(k, z0, z1):
+    def chunk_load(k, pieces):
         sums = jnp.zeros((8, ROWS), jnp.float32)
-        for i, zz in enumerate((z0, z1)):
+        for i, zz in pieces:
             block = xg[:, zz].reshape(LANES, ROWS)
             at = (k - 1) * 2 * LANES + i * LANES
             xb[:, at:at + LANES] = jnp.transpose(block)
@@ -217,7 +218,7 @@
         if k > 1:
             sums += squares[...]
         squares[...] = sums
-        if k == NZ // 2:
+        if k == NZ // 2 and pieces[-1][0] == 1:
             spread_scale(inverse(sums), LOG2E / EPSILON)
 
     def chunk_product(k, z0, z1, slot):
@@ -418,11 +419,14 @@
                 return
             loaded.append(zs)
             share(zs)
-            chunk_load(k, *zs)
+            pieces = list(enumerate(zs))
+            chunk_load(k, pieces[1:] if k == NZ // 2 else pieces)
             for slot in (1, 0) if k >= NZ // 2 - 1 else (1,):
                 chunk_product(k, *zs, slot)
                 if k == NZ // 2:
                     send_columns(0, slot)
+            if k == NZ // 2 - 1:
+                chunk_load(k + 1, [(0, z)])
 
         gather(1, work, go)
         last = SINK_ITERS - 1

time: 61.3 us -> 61.2 us (level)
  no operation moved by 1% of the time
where the time goes in v5:
time: 61.2 us; the launch traced here: 61.1 us
  Pallas kernels  58.6 us (96%)
  local copies, waits for them, and re-layouts  1.91 us (3%)
  between operations  0.64 us (1%)
    pallas_call x1, Pallas kernels, local(): pl.pallas_call(swap_kernel, out_shape=(jax.ShapeDtypeStruct((ROWS, COLS),...  58.6 us
    unnamed x2, local copies, waits for them, and re-layouts  1.91 us

profile of v5, /device:TPU:1, one launch (start us, length us, event | category | flops | bytes accessed | tf_op | source)
XLA Modules:
  0.0 61.1 jit_solution(11283579573645914981)
XLA Ops:
  0.6 58.6 %swapped_sinkhorn.1 = (bf16[1024,1024]{1,0:T(8,128)(2,1)S(1)}, f32[8,128]{1,0:T(8,128)S(1)}) custom-call(bf16[16,1024]{1,0:T(8,128)(2,1)} %bitcast.4, bf16[16,1024]{1,0:T(8,128)(2,1)} %bitcast.5, bf16[1024,1024]{1,0:T(8,128)(2,1)} %p_ref.1), custom_call_target="tpu_custom_call" | custom-call | tf_op jit(solution)/shard_map/swapped_sinkhorn/pallas_call | solution.py:516
  59.2 1.3 %copy.7 = bf16[1024,1024]{1,0:T(8,128)(2,1)} copy(bf16[1024,1024]{1,0:T(8,128)(2,1)S(1)} %get-tuple-element.8) | data formatting | bytes 4194304
  60.5 0.6 copy.8
